TPU v7x, 32 devices: a whole 2x2x4 slice. The times are simulated.
32 devices in a mesh: client: 16 (over z, y, core), tp: 2 (over x).
Axes of the slice: x: 2, y: 2, z: 4, core: 2. Of those that a mesh axis runs over, the one named last changes fastest.
Arguments:
- tokens: bfloat16 [4096, 2048], P('client'), may hold values from -6 to 6
- targets: bfloat16 [4096, 2048], P('client'), may hold values from -6 to 6
- norm_gain: float32 [2048], replicated, may hold values from 0.25 to 1.75
- up_frozen: bfloat16 [2048, 7168], P('client', 'tp'), may hold values from -0.125 to 0.125
- down_frozen: bfloat16 [7168, 2048], P('tp', 'client'), may hold values from -0.0625 to 0.0625
- up_left: float32 [16, 2048], replicated, may hold values from -1 to 1
- up_right: float32 [16, 7168], P(None, 'tp'), may hold values from -0.4375 to 0.4375
- down_left: float32 [16, 7168], P(None, 'tp'), may hold values from -0.625 to 0.625
- down_right: float32 [16, 2048], replicated, may hold values from -0.0625 to 0.0625
- counts: int32 [16], P('client'), may hold values from 64 to 4096
Outputs:
- round_up_left: float32 [16, 2048], replicated
- round_up_right: float32 [16, 7168], P(None, 'tp')
- round_down_left: float32 [16, 7168], P(None, 'tp')
- round_down_right: float32 [16, 2048], replicated
All inputs are finite; a program needn't handle non-finite values.
Results may differ from a plain program's by a relative error of at most 0.0089.
Values may be sent and summed in bfloat16 or wider, within the bound.
A program may use at most 128 MiB of HBM per device.

v0:
```python
import jax
import jax.numpy as jnp
from jax import lax
from jax.sharding import PartitionSpec as P

STEPS = 3
LEARN_RATE = 0.01
PROX_WEIGHT = 10.0
ADAPTER_SCALING = 0.5
NORM_EPS = 1e-05


def contracted_rows(left, right):
    return lax.dot_general(
        left, right, (((0,), (0,)), ((), ())), preferred_element_type=jnp.float32
    )


def contract_columns(left, right):
    return lax.dot_general(
        left, right, (((1,), (1,)), ((), ())), preferred_element_type=jnp.float32
    )


def update(value, grad, anchor):
    return value - LEARN_RATE * (grad + PROX_WEIGHT * (value - anchor))


def per_device(
    tokens,
    targets,
    norm_gain,
    up_frozen,
    down_frozen,
    up_left,
    up_right,
    down_left,
    down_right,
    counts,
):
    token_count = tokens.shape[0]
    wide = tokens.astype(jnp.float32)
    scale = lax.rsqrt(jnp.mean(wide * wide, axis=1, keepdims=True) + NORM_EPS)
    normalized_input = (wide * scale * norm_gain).astype(jnp.bfloat16)
    whole_up = lax.all_gather(up_frozen, "client", axis=0, tiled=True)
    frozen_hidden_rows = jnp.dot(normalized_input, whole_up, preferred_element_type=jnp.float32)
    whole_down = lax.all_gather(down_frozen, "client", axis=1, tiled=True)
    start = (up_left, up_right, down_left, down_right)
    params = start
    for local_step in range(STEPS):
        up_left_b = params[0].astype(jnp.bfloat16)
        up_right_batch = params[1].astype(jnp.bfloat16)
        down_left_b = params[2].astype(jnp.bfloat16)
        down_right_batch = params[3].astype(jnp.bfloat16)
        up_low_product = contract_columns(normalized_input, up_left_b).astype(jnp.bfloat16)
        hidden_preactivation = frozen_hidden_rows + ADAPTER_SCALING * jnp.dot(
            up_low_product, up_right_batch, preferred_element_type=jnp.float32
        )
        gated_hidden = jax.nn.silu(hidden_preactivation).astype(jnp.bfloat16)
        partial_value = jnp.dot(gated_hidden, whole_down, preferred_element_type=jnp.float32)
        low_part = contract_columns(gated_hidden, down_left_b)
        share_width = partial_value.shape[1] // lax.axis_size("tp")
        offset = lax.axis_index("tp") * share_width
        summed = lax.psum_scatter(partial_value, "tp", scatter_dimension=1, tiled=True)
        down_low_product = lax.psum(low_part, "tp").astype(jnp.bfloat16)
        right_share = lax.dynamic_slice_in_dim(down_right_batch, offset, share_width, 1)
        token_share = lax.dynamic_slice_in_dim(tokens, offset, share_width, 1)
        target_share = lax.dynamic_slice_in_dim(targets, offset, share_width, 1)
        layer_output = token_share.astype(jnp.float32) + summed
        layer_output = layer_output + ADAPTER_SCALING * jnp.dot(
            down_low_product, right_share, preferred_element_type=jnp.float32
        )
        d_share = ((layer_output - target_share.astype(jnp.float32)) / token_count).astype(
            jnp.bfloat16
        )
        output_gradient = lax.all_gather(d_share, "tp", axis=1, tiled=True)
        down_low_gradient = (
            ADAPTER_SCALING * contract_columns(output_gradient, down_right_batch)
        ).astype(jnp.bfloat16)
        d_gated = contract_columns(output_gradient, whole_down) + jnp.dot(
            down_low_gradient, down_left_b, preferred_element_type=jnp.float32
        )
        sigmoid_pre = jax.nn.sigmoid(hidden_preactivation)
        hidden_gradient = (
            d_gated * sigmoid_pre * (1.0 + hidden_preactivation * (1.0 - sigmoid_pre))
        ).astype(jnp.bfloat16)
        low_rank_gradient = lax.psum(
            ADAPTER_SCALING * contract_columns(hidden_gradient, up_right_batch), "tp"
        )
        up_low_gradient = low_rank_gradient.astype(jnp.bfloat16)
        gradient_tree = (
            contracted_rows(up_low_gradient, normalized_input),
            ADAPTER_SCALING * contracted_rows(up_low_product, hidden_gradient),
            contracted_rows(down_low_gradient, gated_hidden),
            ADAPTER_SCALING * contracted_rows(down_low_product, output_gradient),
        )
        params = jax.tree.map(update, params, gradient_tree, start)
    weight = counts.astype(jnp.float32)

    def weighted(anchor, value):
        return weight[0] * (anchor - value)

    deltas = jax.tree.map(weighted, start, params)
    sums = lax.psum((deltas[0], deltas[1], deltas[2], deltas[3], weight), "client")
    factor = LEARN_RATE * sums[4][0]
    return (sums[0] / factor, sums[1] / factor, sums[2] / factor, sums[3] / factor)


def solution(mesh):
    placed = (
        P("client", None),
        P("client", None),
        P(),
        P("client", "tp"),
        P("tp", "client"),
        P(),
        P(None, "tp"),
        P(None, "tp"),
        P(),
        P("client"),
    )
    return jax.shard_map(
        per_device,
        mesh=mesh,
        in_specs=placed,
        out_specs=(P(), P(None, "tp"), P(None, "tp"), P()),
        check_vma=False,
    )
```

profile of v0, /device:TPU:0, one launch (start us, length us, event | category | flops | bytes accessed | tf_op | source)
XLA Modules:
  0.0 624.4 jit_solution(11934358948694620464)
XLA Ops:
  7.2 0.7 all-gather.6.cloned.1.call-update
  8.0 0.7 all-gather.8.cloned.1.call-update
  8.7 1.5 fusion.50
  10.2 1.7 convolution_convert_fusion.2
  11.9 114.4 %all-gather.6.cloned.1.call-done = bf16[2048,3584]{1,0:T(8,128)(2,1)} async-done(((bf16[128,3584]{1,0:T(8,128)(2,1)}), bf16[2048,3584]{1,0:T(8,128)(2,1)}) %all-gather.6.cloned.1.call-update) | async-done | bytes 14680080 | tf_op jit(solution)/shard_map/all_gather | solution.py:45
  126.4 7.4 %fusion.104 = f32[256,3584]{1,0:T(8,128)S(1)} fusion(bf16[2048,3584]{1,0:T(8,128)(2,1)} %all-gather.6.cloned.1.call-done, bf16[256,2048]{1,0:T(8,128)(2,1)S(1)} %copy-done.3, f32[2048]{0:T(1024)S(1)} %copy-done.30, f32[256]{0:T(256)S(1)} %add_rsqrt_fusion), kind=kOutput, calls=%fused_computation.147 | convolution fusion | flops 3760193536 | bytes 19407872 | tf_op jit(solution)/shard_map/dot_general | solution.py:46
  133.8 1.8 copy-done.37
  135.6 3.1 multiply_convert_fusion.2
  138.7 104.7 %all-gather.8.cloned.1.call-done = bf16[3584,2048]{1,0:T(8,128)(2,1)} async-done(((bf16[3584,128]{1,0:T(8,128)(2,1)}), bf16[3584,2048]{1,0:T(8,128)(2,1)}) %all-gather.8.cloned.1.call-update) | async-done | bytes 14680080 | tf_op jit(solution)/shard_map/all_gather | solution.py:47
  243.4 8.8 %fusion.108 = f32[256,2048]{1,0:T(8,128)} fusion(bf16[256,3584]{1,0:T(8,128)(2,1)S(1)} %get-tuple-element.8, bf16[3584,2048]{1,0:T(8,128)(2,1)} %all-gather.8.cloned.1.call-done), kind=kOutput, calls=%fused_computation.150 | convolution fusion | flops 3758096384 | bytes 18612224 | tf_op jit(solution)/shard_map/dot_general | solution.py:60
  252.3 1.2 fusion.79
  253.5 9.4 %psum.77 = bf16[256,16]{0,1:T(8,128)(2,1)S(1)} all-reduce(f32[256,16]{0,1:T(8,128)} %fusion.79), channel_id=1, replica_groups=mesh['client'=16,'tp'=2] {'tp'}, use_global_device_ids=true, to_apply=%region_2.3 | all-reduce | flops 4096 | bytes 24576 | tf_op jit(solution)/shard_map/psum | solution.py:65
  262.9 19.8 %reduce-scatter.4.cloned.1.call-done = f32[256,1024]{1,0:T(8,128)} async-done(((f32[256,2048]{1,0:T(8,128)}), f32[256,1024]{1,0:T(8,128)}) %reduce-scatter.4.cloned.1.call-update) | async-done | bytes 1048592 | tf_op jit(solution)/shard_map/reduce_scatter | solution.py:64
  282.7 2.5 fusion.59
  285.3 21.2 %all-gather.10.cloned.1.call-done = bf16[256,2048]{1,0:T(8,128)(2,1)} async-done(((bf16[256,1024]{1,0:T(8,128)(2,1)}), bf16[256,2048]{1,0:T(8,128)(2,1)}) %all-gather.10.cloned.1.call-update) | async-done | bytes 1048592 | tf_op jit(solution)/shard_map/all_gather | solution.py:76
  306.5 9.5 %fusion.109 = f32[256,3584]{1,0:T(8,128)S(1)} fusion(bf16[256,2048]{1,0:T(8,128)(2,1)} %all-gather.10.cloned.1.call-done, bf16[3584,2048]{1,0:T(8,128)(2,1)} %all-gather.8.cloned.1.call-done), kind=kOutput, calls=%fused_computation.151 | convolution fusion | flops 3758096384 | bytes 19398656 | tf_op jit(solution)/shard_map/dot_general | solution.py:20
  316.4 3.7 fusion.9
  320.1 1.1 fusion.30
  321.2 0.6 convolution_multiply_fusion.16
  321.7 7.0 %psum.78 = bf16[256,16]{0,1:T(8,128)(2,1)S(1)} all-reduce(f32[256,16]{0,1:T(8,128)S(1)} %convolution_multiply_fusion.16), channel_id=1, replica_groups=mesh['client'=16,'tp'=2] {'tp'}, use_global_device_ids=true, to_apply=%region_3.4 | all-reduce | flops 4096 | bytes 24576 | tf_op jit(solution)/shard_map/psum | solution.py:87
  329.2 0.7 copy-done.36
  330.3 0.7 copy-done.38
  331.0 3.1 multiply_convert_fusion.1
  334.1 8.7 %fusion.110 = f32[256,2048]{1,0:T(8,128)} fusion(bf16[256,3584]{1,0:T(8,128)(2,1)S(1)} %get-tuple-element.10, bf16[3584,2048]{1,0:T(8,128)(2,1)} %all-gather.8.cloned.1.call-done), kind=kOutput, calls=%fused_computation.152 | convolution fusion | flops 3758096384 | bytes 18612224 | tf_op jit(solution)/shard_map/dot_general | solution.py:60
  342.8 1.9 fusion.27
  344.7 0.7 copy-done.9
  345.4 0.6 fusion.74
  345.9 8.8 %psum.79 = bf16[256,16]{0,1:T(8,128)(2,1)S(1)} all-reduce(f32[256,16]{0,1:T(8,128)S(1)} %fusion.74), channel_id=1, replica_groups=mesh['client'=16,'tp'=2] {'tp'}, use_global_device_ids=true, to_apply=%region_5.6 | all-reduce | flops 4096 | bytes 24576 | tf_op jit(solution)/shard_map/psum | solution.py:65
  354.7 2.1 fusion.106
  356.9 19.2 %reduce-scatter.6.cloned.1.call-done = f32[256,1024]{1,0:T(8,128)} async-done(((f32[256,2048]{1,0:T(8,128)}), f32[256,1024]{1,0:T(8,128)}) %reduce-scatter.6.cloned.1.call-update) | async-done | bytes 1048592 | tf_op jit(solution)/shard_map/reduce_scatter | solution.py:64
  376.1 2.6 fusion.60
  378.8 21.5 %all-gather.12.cloned.1.call-done = bf16[256,2048]{1,0:T(8,128)(2,1)} async-done(((bf16[256,1024]{1,0:T(8,128)(2,1)}), bf16[256,2048]{1,0:T(8,128)(2,1)}) %all-gather.12.cloned.1.call-update) | async-done | bytes 1048592 | tf_op jit(solution)/shard_map/all_gather | solution.py:76
  400.2 1.6 fusion.63
  401.8 7.6 %fusion.111 = f32[256,3584]{1,0:T(8,128)S(1)} fusion(bf16[256,2048]{1,0:T(8,128)(2,1)} %all-gather.12.cloned.1.call-done, bf16[3584,2048]{1,0:T(8,128)(2,1)} %all-gather.8.cloned.1.call-done), kind=kOutput, calls=%fused_computation.153 | convolution fusion | flops 3758096384 | bytes 19398656 | tf_op jit(solution)/shard_map/dot_general | solution.py:20
  409.5 3.7 fusion.10
  413.3 1.1 fusion.25
  414.3 0.6 convolution_multiply_fusion.14
  414.9 7.0 %psum.80 = bf16[256,16]{0,1:T(8,128)(2,1)S(1)} all-reduce(f32[256,16]{0,1:T(8,128)S(1)} %convolution_multiply_fusion.14), channel_id=1, replica_groups=mesh['client'=16,'tp'=2] {'tp'}, use_global_device_ids=true, to_apply=%region_6.7 | all-reduce | flops 4096 | bytes 24576 | tf_op jit(solution)/shard_map/psum | solution.py:87
  422.0 1.5 fusion.44
  423.5 0.7 copy-done.34
  424.6 3.0 multiply_convert_fusion
  427.7 1.3 copy-done.1
  428.9 8.7 %fusion.112 = f32[256,2048]{1,0:T(8,128)} fusion(bf16[256,3584]{1,0:T(8,128)(2,1)S(1)} %get-tuple-element.14, bf16[3584,2048]{1,0:T(8,128)(2,1)} %all-gather.8.cloned.1.call-done), kind=kOutput, calls=%fused_computation.154 | convolution fusion | flops 3758096384 | bytes 18612224 | tf_op jit(solution)/shard_map/dot_general | solution.py:60
  437.7 1.3 fusion.22
  439.0 0.7 copy-done.15
  439.7 2.2 fusion.69
  441.9 8.9 %psum.81 = bf16[256,16]{0,1:T(8,128)(2,1)S(1)} all-reduce(f32[256,16]{0,1:T(8,128)S(1)} %fusion.69), channel_id=1, replica_groups=mesh['client'=16,'tp'=2] {'tp'}, use_global_device_ids=true, to_apply=%region_8.9 | all-reduce | flops 4096 | bytes 24576 | tf_op jit(solution)/shard_map/psum | solution.py:65
  450.8 2.1 fusion.107
  452.9 18.1 %reduce-scatter.8.cloned.1.call-done = f32[256,1024]{1,0:T(8,128)} async-done(((f32[256,2048]{1,0:T(8,128)}), f32[256,1024]{1,0:T(8,128)}) %reduce-scatter.8.cloned.1.call-update) | async-done | bytes 1048592 | tf_op jit(solution)/shard_map/reduce_scatter | solution.py:64
  471.0 2.6 fusion.61
  474.3 20.8 %all-gather.14.cloned.1.call-done = bf16[256,2048]{1,0:T(8,128)(2,1)} async-done(((bf16[256,1024]{1,0:T(8,128)(2,1)}), bf16[256,2048]{1,0:T(8,128)(2,1)}) %all-gather.14.cloned.1.call-update) | async-done | bytes 1048592 | tf_op jit(solution)/shard_map/all_gather | solution.py:76
  495.1 1.6 fusion.64
  496.7 2.0 fusion.15
  498.7 7.6 %fusion.113 = f32[256,3584]{1,0:T(8,128)S(1)} fusion(bf16[256,2048]{1,0:T(8,128)(2,1)} %all-gather.14.cloned.1.call-done, bf16[3584,2048]{1,0:T(8,128)(2,1)} %all-gather.8.cloned.1.call-done), kind=kOutput, calls=%fused_computation.155 | convolution fusion | flops 3758096384 | bytes 19398656 | tf_op jit(solution)/shard_map/dot_general | solution.py:20
  506.4 3.7 fusion.11
  510.2 1.1 fusion.20
  511.2 0.6 convolution_multiply_fusion.12
  511.8 7.0 %psum.82 = bf16[256,16]{0,1:T(8,128)(2,1)S(1)} all-reduce(f32[256,16]{0,1:T(8,128)S(1)} %convolution_multiply_fusion.12), channel_id=1, replica_groups=mesh['client'=16,'tp'=2] {'tp'}, use_global_device_ids=true, to_apply=%region_9.10 | all-reduce | flops 4096 | bytes 24576 | tf_op jit(solution)/shard_map/psum | solution.py:87
  518.8 1.1 fusion.39
  519.9 0.9 fusion.35
  520.9 32.8 %psum.84 = f32[1]{0:T(128)} all-reduce(f32[1]{0:T(128)} %convert_element_type.118), channel_id=1, replica_groups=mesh['client'=16,'tp'=2] {'client'}, use_global_device_ids=true, to_apply=%region_11.12 | all-reduce | flops 1 | bytes 8 | tf_op jit(solution)/shard_map/psum | solution.py:104
  554.4 60.0 %all-reduce.3.cloned.1.call-done = (f32[16,2048]{1,0:T(8,128)}, f32[16,3584]{1,0:T(8,128)}, f32[16,3584]{1,0:T(8,128)}, f32[16,2048]{1,0:T(8,128)}) async-done(((f32[16,2048]{1,0:T(8,128)}, f32[16,3584]{1,0:T(8,128)}, f32[16,3584]{1,0:T(8,128)}, f32[16,2048]{1,0:T(8,128)}), (f32[16,2048]{1,0:T(8,128)}, f32[16,3584]{1,0:T(8,128)}, f32[16,3584]{1,0:T(8,128)}, ...) | async-done | bytes 720912 | tf_op jit(solution)/shard_map/psum | solution.py:104
  614.3 1.8 broadcast_divide_fusion
  616.2 1.7 broadcast_divide_fusion.2
  (95 shorter events, 2.4 us)
Async XLA Ops:
  7.2 119.2 %copy-start.3 = (bf16[256,2048]{1,0:T(8,128)(2,1)S(1)}, bf16[256,2048]{1,0:T(8,128)(2,1)}, u32[]{:S(2)}) copy-start(bf16[256,2048]{1,0:T(8,128)(2,1)} %param.10) | copy-start | bytes 3145732
  7.2 119.2 %copy-start.30 = (f32[2048]{0:T(1024)S(1)}, f32[2048]{0:T(1024)}, u32[]{:S(2)}) copy-start(f32[2048]{0:T(1024)} %param.12) | copy-start | bytes 24580
  7.2 119.2 %all-gather.6.cloned.1.call-start = ((), (), s32[]{:S(2)}) async-start(), calls=%async_computation.3 | async-start | bytes 15597568 | tf_op jit(solution)/shard_map/all_gather | solution.py:45
  7.9 235.5 %all-gather.8.cloned.1.call-start = ((), (), s32[]{:S(2)}) async-start(), calls=%async_computation.4 | async-start | bytes 15597568 | tf_op jit(solution)/shard_map/all_gather | solution.py:47
  8.7 274.0 %reduce-scatter.4.cloned.1.call-start = ((), (), s32[]{:S(2)}) async-start(), calls=%async_computation.5 | async-start | bytes 3145728 | tf_op jit(solution)/shard_map/reduce_scatter | solution.py:64
  10.2 123.5 %copy-start.24 = (f32[256]{0:T(256)}, f32[256]{0:T(256)S(1)}, u32[]{:S(2)}) copy-start(f32[256]{0:T(256)S(1)} %add_rsqrt_fusion) | copy-start | bytes 3076
  11.9 121.8 %copy-start.18 = (bf16[256,16]{0,1:T(8,128)(2,1)}, bf16[256,16]{0,1:T(8,128)(2,1)S(1)}, u32[]{:S(2)}) copy-start(bf16[256,16]{0,1:T(8,128)(2,1)S(1)} %convolution_convert_fusion.2) | copy-start | bytes 24580
  11.9 123.7 %copy-start.7 = (f32[16,3584]{1,0:T(8,128)S(1)}, f32[16,3584]{1,0:T(8,128)}, u32[]{:S(2)}) copy-start(f32[16,3584]{1,0:T(8,128)} %param.16) | copy-start | bytes 688132
  133.8 1.8 copy-start.37
  138.7 113.6 %copy-start = (bf16[256,3584]{1,0:T(8,128)(2,1)}, bf16[256,3584]{1,0:T(8,128)(2,1)S(1)}, u32[]{:S(2)}) copy-start(bf16[256,3584]{1,0:T(8,128)(2,1)S(1)} %get-tuple-element.8) | copy-start | bytes 5505028
  243.4 8.8 %copy-start.8 = (f32[16,2048]{1,0:T(8,128)S(1)}, f32[16,2048]{1,0:T(8,128)}, u32[]{:S(2)}) copy-start(f32[16,2048]{1,0:T(8,128)} %param.18) | copy-start | bytes 393220
  243.4 8.9 %copy-start.6 = (f32[16,3584]{1,0:T(8,128)S(1)}, f32[16,3584]{1,0:T(8,128)}, u32[]{:S(2)}) copy-start(f32[16,3584]{1,0:T(8,128)} %param.17) | copy-start | bytes 688132
  252.2 54.3 %all-gather.10.cloned.1.call-start = ((), (), s32[]{:S(2)}) async-start(), calls=%async_computation.6 | async-start | bytes 1572864 | tf_op jit(solution)/shard_map/all_gather | solution.py:76
  285.2 90.9 %reduce-scatter.6.cloned.1.call-start = ((), (), s32[]{:S(2)}) async-start(), calls=%async_computation.7 | async-start | bytes 3145728 | tf_op jit(solution)/shard_map/reduce_scatter | solution.py:64
  306.5 9.5 %copy-start.4 = (bf16[256,2048]{1,0:T(8,128)(2,1)S(1)}, bf16[256,2048]{1,0:T(8,128)(2,1)}, u32[]{:S(2)}) copy-start(bf16[256,2048]{1,0:T(8,128)(2,1)} %all-gather.10.cloned.1.call-done) | copy-start | bytes 3145732
  316.4 3.7 copy-start.19
  320.1 8.7 %copy-start.25 = (f32[256]{0:T(256)S(1)}, f32[256]{0:T(256)}, u32[]{:S(2)}) copy-start(f32[256]{0:T(256)} %copy-done.24) | copy-start | bytes 3076
  320.1 8.7 %copy-start.28 = (f32[16,2048]{1,0:T(8,128)S(1)}, f32[16,2048]{1,0:T(8,128)}, u32[]{:S(2)}) copy-start(f32[16,2048]{1,0:T(8,128)} %param.15) | copy-start | bytes 393220
  320.1 8.7 %copy-start.31 = (f32[2048]{0:T(1024)S(1)}, f32[2048]{0:T(1024)}, u32[]{:S(2)}) copy-start(f32[2048]{0:T(1024)} %param.12) | copy-start | bytes 24580
  328.8 1.6 copy-start.11
  328.8 2.2 copy-start.38
  329.2 0.7 copy-start.36
  331.0 3.1 copy-start.22
  342.8 57.5 %all-gather.12.cloned.1.call-start = ((), (), s32[]{:S(2)}) async-start(), calls=%async_computation.8 | async-start | bytes 1572864 | tf_op jit(solution)/shard_map/all_gather | solution.py:76
  344.7 0.7 copy-start.9
  378.7 92.3 %reduce-scatter.8.cloned.1.call-start = ((), (), s32[]{:S(2)}) async-start(), calls=%async_computation.9 | async-start | bytes 3145728 | tf_op jit(solution)/shard_map/reduce_scatter | solution.py:64
  401.8 7.7 %copy-start.10 = (f32[16,3584]{1,0:T(8,128)S(1)}, f32[16,3584]{1,0:T(8,128)}, u32[]{:S(2)}) copy-start(f32[16,3584]{1,0:T(8,128)} %copy-done.9) | copy-start | bytes 688132
  409.5 3.7 copy-start.12
  409.5 3.7 copy-start.23
  413.3 8.7 %copy-start.26 = (f32[256]{0:T(256)S(1)}, f32[256]{0:T(256)}, u32[]{:S(2)}) copy-start(f32[256]{0:T(256)} %copy-done.24) | copy-start | bytes 3076
  413.3 8.7 %copy-start.32 = (f32[2048]{0:T(1024)S(1)}, f32[2048]{0:T(1024)}, u32[]{:S(2)}) copy-start(f32[2048]{0:T(1024)} %param.12) | copy-start | bytes 24580
  421.9 2.7 copy-start.13
  421.9 2.7 copy-start.39
  423.5 0.7 copy-start.34
  424.6 3.1 copy-start.20
  427.7 1.3 copy-start.1
  437.7 57.4 %all-gather.14.cloned.1.call-start = ((), (), s32[]{:S(2)}) async-start(), calls=%async_computation.10 | async-start | bytes 1572864 | tf_op jit(solution)/shard_map/all_gather | solution.py:76
  439.0 0.7 copy-start.15
  439.7 57.0 %copy-start.2 = (bf16[256,3584]{1,0:T(8,128)(2,1)S(1)}, bf16[256,3584]{1,0:T(8,128)(2,1)}, u32[]{:S(2)}) copy-start(bf16[256,3584]{1,0:T(8,128)(2,1)} %copy-done.1) | copy-start | bytes 5505028
  473.6 140.7 %all-reduce.3.cloned.1.call-start = ((), (), s32[]{:S(2)}) async-start(), calls=%async_computation.11 | async-start | bytes 1441792 | tf_op jit(solution)/shard_map/psum | solution.py:104
  498.7 7.6 %copy-start.16 = (f32[16,3584]{1,0:T(8,128)S(1)}, f32[16,3584]{1,0:T(8,128)}, u32[]{:S(2)}) copy-start(f32[16,3584]{1,0:T(8,128)} %copy-done.15) | copy-start | bytes 688132
  506.4 3.7 copy-start.14
  506.4 3.7 copy-start.21
  510.1 8.7 %copy-start.27 = (f32[256]{0:T(256)S(1)}, f32[256]{0:T(256)}, u32[]{:S(2)}) copy-start(f32[256]{0:T(256)} %copy-done.24) | copy-start | bytes 3076
  510.1 8.7 %copy-start.29 = (f32[16,2048]{1,0:T(8,128)S(1)}, f32[16,2048]{1,0:T(8,128)}, u32[]{:S(2)}) copy-start(f32[16,2048]{1,0:T(8,128)} %param.15) | copy-start | bytes 393220
  510.1 8.7 %copy-start.33 = (f32[2048]{0:T(1024)S(1)}, f32[2048]{0:T(1024)}, u32[]{:S(2)}) copy-start(f32[2048]{0:T(1024)} %param.12) | copy-start | bytes 24580
  510.1 8.7 %copy-start.35 = (f32[16,2048]{1,0:T(8,128)S(1)}, f32[16,2048]{1,0:T(8,128)}, u32[]{:S(2)}) copy-start(f32[16,2048]{1,0:T(8,128)} %copy-done.34) | copy-start | bytes 393220
  510.2 9.8 %copy-start.5 = (bf16[256,2048]{1,0:T(8,128)(2,1)S(1)}, bf16[256,2048]{1,0:T(8,128)(2,1)}, u32[]{:S(2)}) copy-start(bf16[256,2048]{1,0:T(8,128)(2,1)} %all-gather.14.cloned.1.call-done) | copy-start | bytes 3145732
  510.2 9.8 %copy-start.17 = (f32[16,2048]{1,0:T(8,128)S(1)}, f32[16,2048]{1,0:T(8,128)}, u32[]{:S(2)}) copy-start(f32[16,2048]{1,0:T(8,128)} %get-tuple-element.17) | copy-start | bytes 393220
Sparse Core Ops, SparseCore 0:
  10.3 116.0 all-gather.5
  128.5 114.8 all-gather.7
  252.3 30.3 reduce-scatter.3
  285.4 21.0 all-gather.9
  342.9 33.1 reduce-scatter.5
  378.8 21.3 all-gather.11
  437.8 33.1 reduce-scatter.7
  473.7 21.3 all-gather.13
  521.0 93.3 all-reduce.2
where the time goes:
time: 625 us; the launch traced here: 624 us
  waiting for transfers between devices  401 us (64%)
  matrix products  115 us (18%)
  blocking collectives  81 us (13%)
  between operations  15.6 us (2%)
  local copies, waits for them, and re-layouts  6.61 us (1%)
    all_gather x1, waiting for transfers between devices, per_device(): whole_up = lax.all_gather(up_frozen, 'client', axis=0, tiled=True)  114 us
    all_gather x1, waiting for transfers between devices, per_device(): whole_down = lax.all_gather(down_frozen, 'client', axis=1, tiled=True)  105 us
    all_gather x3, waiting for transfers between devices, per_device(): output_gradient = lax.all_gather(d_share, 'tp', axis=1, tiled=True)  63.5 us
    psum x1, waiting for transfers between devices, per_device(): lax.psum((deltas[0], deltas[1], deltas[2], deltas[3], weight), 'client')  60 us
    reduce_scatter x3, waiting for transfers between devices, per_device(): lax.psum_scatter(partial_value, 'tp', scatter_dimension=1, tiled=True)  57.1 us
    dot_general x15, matrix products, contract_columns(): lax.dot_general(left, right, (((1,), (1,)), ((), ())), preferred_element_...  36.5 us
    psum x1, blocking collectives, per_device(): lax.psum((deltas[0], deltas[1], deltas[2], deltas[3], weight), 'client')  32.8 us
    psum x3, blocking collectives, per_device(): down_low_product = lax.psum(low_part, 'tp').astype(jnp.bfloat16)  27.1 us
  transfers between devices with their start and end apart: 9, of which 9 were waited for; matrix products, arithmetic and copies ran while one was open for 4% of the time, Pallas kernels for 0%

commit v1 on v0

--- a/solution.py
+++ b/solution.py
@@ -44,7 +44,14 @@
     normalized_input = (wide * scale * norm_gain).astype(jnp.bfloat16)
     whole_up = lax.all_gather(up_frozen, "client", axis=0, tiled=True)
     frozen_hidden_rows = jnp.dot(normalized_input, whole_up, preferred_element_type=jnp.float32)
-    whole_down = lax.all_gather(down_frozen, "client", axis=1, tiled=True)
+    ring = [down_frozen]
+    for hop in range(15):
+        ring.append(lax.ppermute(ring[-1], "client", [(dev, (dev + 1) % 16) for dev in range(16)]))
+    whole_down = jnp.roll(
+        jnp.concatenate(ring[::-1], axis=1),
+        (lax.axis_index("client") + 1) * ring[0].shape[1],
+        axis=1,
+    )
     start = (up_left, up_right, down_left, down_right)
     params = start
     for local_step in range(STEPS):

time: 625 us -> 774 us (1.24); the launches traced: 624 us -> 765 us
  waiting for transfers between devices: 401 us -> 473 us
  local copies, waits for them, and re-layouts: 6.61 us -> 51.6 us
  matrix products: 115 us -> 127 us
  other arithmetic: 5.07 us -> 12.9 us
    ppermute x0 -> x15, waiting for transfers between devices: none -> 294 us  [per_device(): lax.ppermute(ring[-1], 'client', [(dev, (dev + 1) % 16) for dev in range(...]
    all_gather x1, waiting for transfers between devices: 114 us -> 0.01 us  [per_device(): whole_up = lax.all_gather(up_frozen, 'client', axis=0, tiled=True)]
    all_gather x1 -> x0, waiting for transfers between devices: 105 us -> none  [per_device(): whole_down = lax.all_gather(down_frozen, 'client', axis=1, tiled=True)]
    unnamed x80 -> x145, local copies, waits for them, and re-layouts: 6.61 us -> 50.6 us
    dot_general x15, matrix products: 36.5 us -> 51.9 us  [contract_columns(): lax.dot_general(left, right, (((1,), (1,)), ((), ())), preferred_element_...]
    convert_element_type x0 -> x3, other arithmetic: none -> 7.76 us  [per_device(): ((layer_output - target_share.astype(jnp.float32)) / token_count).astype(...]
  transfers between devices with their start and end apart: 9 -> 23, of which waited for: 9 -> 22; matrix products, arithmetic and copies ran while one was open for 4% -> 7% of each run, Pallas kernels for 0% -> 0%
where the time goes in v1:
time: 774 us; the launch traced here: 765 us
  waiting for transfers between devices  473 us (61%)
  matrix products  127 us (16%)
  blocking collectives  83.4 us (11%)
  local copies, waits for them, and re-layouts  51.6 us (7%)
  between operations  16.1 us (2%)
  other arithmetic  12.9 us (2%)
    ppermute x15, waiting for transfers between devices, per_device(): lax.ppermute(ring[-1], 'client', [(dev, (dev + 1) % 16) for dev in range(...  294 us
    all_gather x3, waiting for transfers between devices, per_device(): output_gradient = lax.all_gather(d_share, 'tp', axis=1, tiled=True)  62.6 us
    psum x1, waiting for transfers between devices, per_device(): lax.psum((deltas[0], deltas[1], deltas[2], deltas[3], weight), 'client')  60 us
    reduce_scatter x3, waiting for transfers between devices, per_device(): lax.psum_scatter(partial_value, 'tp', scatter_dimension=1, tiled=True)  55.5 us
    dot_general x15, matrix products, contract_columns(): lax.dot_general(left, right, (((1,), (1,)), ((), ())), preferred_element_...  51.9 us
    unnamed x145, local copies, waits for them, and re-layouts  50.6 us
    psum x1, blocking collectives, per_device(): lax.psum((deltas[0], deltas[1], deltas[2], deltas[3], weight), 'client')  32.9 us
    psum x3, blocking collectives, per_device(): down_low_product = lax.psum(low_part, 'tp').astype(jnp.bfloat16)  29.4 us
  transfers between devices with their start and end apart: 23, of which 22 were waited for; matrix products, arithmetic and copies ran while one was open for 7% of the time, Pallas kernels for 0%

profile of v1, /device:TPU:0, one launch (start us, length us, event | category | flops | bytes accessed | tf_op | source)
XLA Modules:
  0.0 765.4 jit_solution(12327661754922091802)
XLA Ops:
  7.8 16.3 %collective-permute-done = bf16[3584,128]{1,0:T(8,128)(2,1)S(1)} collective-permute-done((bf16[3584,128]{1,0:T(8,128)(2,1)}, bf16[3584,128]{1,0:T(8,128)(2,1)S(1)}, u32[]{:S(2)}, u32[]{:S(2)}) %collective-permute-start) | collective-permute-done | bytes 917536 | tf_op jit(solution)/shard_map/ppermute | solution.py:49
  24.1 15.6 %collective-permute-done.1 = bf16[3584,128]{1,0:T(8,128)(2,1)S(1)} collective-permute-done((bf16[3584,128]{1,0:T(8,128)(2,1)S(1)}, bf16[3584,128]{1,0:T(8,128)(2,1)S(1)}, u32[]{:S(2)}, u32[]{:S(2)}) %collective-permute-start.1) | collective-permute-done | bytes 917536 | tf_op jit(solution)/shard_map/ppermute | solution.py:49
  39.7 35.3 %collective-permute-done.2 = bf16[3584,128]{1,0:T(8,128)(2,1)S(1)} collective-permute-done((bf16[3584,128]{1,0:T(8,128)(2,1)S(1)}, bf16[3584,128]{1,0:T(8,128)(2,1)S(1)}, u32[]{:S(2)}, u32[]{:S(2)}) %collective-permute-start.2) | collective-permute-done | bytes 917536 | tf_op jit(solution)/shard_map/ppermute | solution.py:49
  75.0 22.2 %collective-permute-done.3 = bf16[3584,128]{1,0:T(8,128)(2,1)S(1)} collective-permute-done((bf16[3584,128]{1,0:T(8,128)(2,1)S(1)}, bf16[3584,128]{1,0:T(8,128)(2,1)S(1)}, u32[]{:S(2)}, u32[]{:S(2)}) %collective-permute-start.3) | collective-permute-done | bytes 917536 | tf_op jit(solution)/shard_map/ppermute | solution.py:49
  98.1 35.3 %collective-permute-done.4 = bf16[3584,128]{1,0:T(8,128)(2,1)S(1)} collective-permute-done((bf16[3584,128]{1,0:T(8,128)(2,1)S(1)}, bf16[3584,128]{1,0:T(8,128)(2,1)S(1)}, u32[]{:S(2)}, u32[]{:S(2)}) %collective-permute-start.4) | collective-permute-done | bytes 917536 | tf_op jit(solution)/shard_map/ppermute | solution.py:49
  134.4 33.1 %collective-permute-done.5 = bf16[3584,128]{1,0:T(8,128)(2,1)S(1)} collective-permute-done((bf16[3584,128]{1,0:T(8,128)(2,1)S(1)}, bf16[3584,128]{1,0:T(8,128)(2,1)S(1)}, u32[]{:S(2)}, u32[]{:S(2)}) %collective-permute-start.5) | collective-permute-done | bytes 917536 | tf_op jit(solution)/shard_map/ppermute | solution.py:49
  168.4 15.5 %collective-permute-done.6 = bf16[3584,128]{1,0:T(8,128)(2,1)S(1)} collective-permute-done((bf16[3584,128]{1,0:T(8,128)(2,1)S(1)}, bf16[3584,128]{1,0:T(8,128)(2,1)S(1)}, u32[]{:S(2)}, u32[]{:S(2)}) %collective-permute-start.6) | collective-permute-done | bytes 917536 | tf_op jit(solution)/shard_map/ppermute | solution.py:49
  184.8 15.5 %collective-permute-done.7 = bf16[3584,128]{1,0:T(8,128)(2,1)S(1)} collective-permute-done((bf16[3584,128]{1,0:T(8,128)(2,1)S(1)}, bf16[3584,128]{1,0:T(8,128)(2,1)S(1)}, u32[]{:S(2)}, u32[]{:S(2)}) %collective-permute-start.7) | collective-permute-done | bytes 917536 | tf_op jit(solution)/shard_map/ppermute | solution.py:49
  201.3 15.5 %collective-permute-done.8 = bf16[3584,128]{1,0:T(8,128)(2,1)S(1)} collective-permute-done((bf16[3584,128]{1,0:T(8,128)(2,1)S(1)}, bf16[3584,128]{1,0:T(8,128)(2,1)S(1)}, u32[]{:S(2)}, u32[]{:S(2)}) %collective-permute-start.8) | collective-permute-done | bytes 917536 | tf_op jit(solution)/shard_map/ppermute | solution.py:49
  217.8 15.5 %collective-permute-done.9 = bf16[3584,128]{1,0:T(8,128)(2,1)S(1)} collective-permute-done((bf16[3584,128]{1,0:T(8,128)(2,1)S(1)}, bf16[3584,128]{1,0:T(8,128)(2,1)S(1)}, u32[]{:S(2)}, u32[]{:S(2)}) %collective-permute-start.9) | collective-permute-done | bytes 917536 | tf_op jit(solution)/shard_map/ppermute | solution.py:49
  234.2 15.5 %collective-permute-done.10 = bf16[3584,128]{1,0:T(8,128)(2,1)S(1)} collective-permute-done((bf16[3584,128]{1,0:T(8,128)(2,1)S(1)}, bf16[3584,128]{1,0:T(8,128)(2,1)S(1)}, u32[]{:S(2)}, u32[]{:S(2)}) %collective-permute-start.10) | collective-permute-done | bytes 917536 | tf_op jit(solution)/shard_map/ppermute | solution.py:49
  250.7 15.5 %collective-permute-done.11 = bf16[3584,128]{1,0:T(8,128)(2,1)S(1)} collective-permute-done((bf16[3584,128]{1,0:T(8,128)(2,1)S(1)}, bf16[3584,128]{1,0:T(8,128)(2,1)S(1)}, u32[]{:S(2)}, u32[]{:S(2)}) %collective-permute-start.11) | collective-permute-done | bytes 917536 | tf_op jit(solution)/shard_map/ppermute | solution.py:49
  267.1 15.5 %collective-permute-done.12 = bf16[3584,128]{1,0:T(8,128)(2,1)S(1)} collective-permute-done((bf16[3584,128]{1,0:T(8,128)(2,1)S(1)}, bf16[3584,128]{1,0:T(8,128)(2,1)S(1)}, u32[]{:S(2)}, u32[]{:S(2)}) %collective-permute-start.12) | collective-permute-done | bytes 917536 | tf_op jit(solution)/shard_map/ppermute | solution.py:49
  283.6 15.6 %collective-permute-done.13 = bf16[3584,128]{1,0:T(8,128)(2,1)} collective-permute-done((bf16[3584,128]{1,0:T(8,128)(2,1)S(1)}, bf16[3584,128]{1,0:T(8,128)(2,1)}, u32[]{:S(2)}, u32[]{:S(2)}) %collective-permute-start.13) | collective-permute-done | bytes 917536 | tf_op jit(solution)/shard_map/ppermute | solution.py:49
  299.2 1.6 fusion.89
  300.8 1.8 convolution_convert_fusion.2
  302.6 12.4 %collective-permute-done.14 = bf16[3584,128]{1,0:T(8,128)(2,1)} collective-permute-done((bf16[3584,128]{1,0:T(8,128)(2,1)}, bf16[3584,128]{1,0:T(8,128)(2,1)}, u32[]{:S(2)}, u32[]{:S(2)}) %collective-permute-start.14) | collective-permute-done | bytes 917536 | tf_op jit(solution)/shard_map/ppermute | solution.py:49
  315.0 2.2 constant_dynamic-update-slice_fusion.31
  317.3 2.3 constant_dynamic-update-slice_fusion.30
  334.6 2.2 constant_dynamic-update-slice_fusion.15
  336.8 2.2 constant_dynamic-update-slice_fusion.14
  353.6 7.4 fusion.152
  361.0 3.1 multiply_convert_fusion.2
  364.2 9.4 %fusion.10 = f32[256,2048]{1,0:T(8,128)} fusion(bf16[256,3584]{1,0:T(8,128)(2,1)S(1)} %get-tuple-element.8, bf16[3584,4096]{1,0:T(8,128)(2,1)} %constant_dynamic-update-slice_fusion, s32[]{:T(128)S(6)} %select_n.26), kind=kOutput, calls=%fused_computation.10 | convolution fusion | flops 3758096384 | bytes 18612228 | tf_op jit(solution)/shard_map/dot_general | solution.py:67
  374.3 11.6 %psum.77 = bf16[256,16]{0,1:T(8,128)(2,1)S(1)} all-reduce(f32[256,16]{0,1:T(8,128)S(1)} %fusion.121), channel_id=1, replica_groups=mesh['client'=16,'tp'=2] {'tp'}, use_global_device_ids=true, to_apply=%region_2.3 | all-reduce | flops 4096 | bytes 24576 | tf_op jit(solution)/shard_map/psum | solution.py:72
  386.2 19.7 %reduce-scatter.4.cloned.1.call-done = f32[256,1024]{1,0:T(8,128)} async-done(((f32[256,2048]{1,0:T(8,128)}), f32[256,1024]{1,0:T(8,128)}) %reduce-scatter.4.cloned.1.call-update) | async-done | bytes 1048592 | tf_op jit(solution)/shard_map/reduce_scatter | solution.py:71
  405.9 2.5 fusion.99
  408.9 20.9 %all-gather.7.cloned.1.call-done = bf16[256,2048]{1,0:T(8,128)(2,1)} async-done(((bf16[256,1024]{1,0:T(8,128)(2,1)}), bf16[256,2048]{1,0:T(8,128)(2,1)}) %all-gather.7.cloned.1.call-update) | async-done | bytes 1048592 | tf_op jit(solution)/shard_map/all_gather | solution.py:83
  429.8 1.6 fusion.92
  431.4 2.5 fusion.119
  433.8 12.3 %fusion.48 = bf16[256,3584]{1,0:T(8,128)(2,1)S(1)} fusion(f32[256,3584]{1,0:T(8,128)} %fusion.119, bf16[256,2048]{1,0:T(8,128)(2,1)} %all-gather.7.cloned.1.call-done, bf16[3584,4096]{1,0:T(8,128)(2,1)} %constant_dynamic-update-slice_fusion, s32[]{:T(128)S(6)} %select_n.26, f32[256,3584]{1,0:T(8,128)} %get-tuple-element.9), kind=kOutput, calls=%fused_computation.29 | convolution fusion | flops 3767271424 | bytes 24903684 | tf_op jit(solution)/shard_map/dot_general | solution.py:20
  447.8 7.0 psum.78
  457.4 3.1 multiply_convert_fusion.1
  460.6 8.7 %fusion.6 = f32[256,2048]{1,0:T(8,128)} fusion(bf16[256,3584]{1,0:T(8,128)(2,1)S(1)} %get-tuple-element.12, bf16[3584,4096]{1,0:T(8,128)(2,1)} %constant_dynamic-update-slice_fusion, s32[]{:T(128)S(6)} %select_n.26), kind=kOutput, calls=%fused_computation.6 | convolution fusion | flops 3758096384 | bytes 18612228 | tf_op jit(solution)/shard_map/dot_general | solution.py:67
  469.3 1.9 fusion.66
  472.4 8.8 %psum.79 = bf16[256,16]{0,1:T(8,128)(2,1)S(1)} all-reduce(f32[256,16]{0,1:T(8,128)S(1)} %fusion.115), channel_id=1, replica_groups=mesh['client'=16,'tp'=2] {'tp'}, use_global_device_ids=true, to_apply=%region_5.6 | all-reduce | flops 4096 | bytes 24576 | tf_op jit(solution)/shard_map/psum | solution.py:72
  481.3 2.2 fusion.154
  484.7 17.9 %reduce-scatter.6.cloned.1.call-done = f32[256,1024]{1,0:T(8,128)} async-done(((f32[256,2048]{1,0:T(8,128)}), f32[256,1024]{1,0:T(8,128)}) %reduce-scatter.6.cloned.1.call-update) | async-done | bytes 1048592 | tf_op jit(solution)/shard_map/reduce_scatter | solution.py:71
  502.6 2.8 fusion.101
  505.7 21.3 %all-gather.9.cloned.1.call-done = bf16[256,2048]{1,0:T(8,128)(2,1)} async-done(((bf16[256,1024]{1,0:T(8,128)(2,1)}), bf16[256,2048]{1,0:T(8,128)(2,1)}) %all-gather.9.cloned.1.call-update) | async-done | bytes 1048592 | tf_op jit(solution)/shard_map/all_gather | solution.py:83
  527.0 1.6 fusion.93
  528.6 3.4 fusion.113
  532.0 13.5 %fusion.45 = bf16[256,3584]{1,0:T(8,128)(2,1)} fusion(f32[256,3584]{1,0:T(8,128)} %fusion.113, bf16[256,2048]{1,0:T(8,128)(2,1)} %all-gather.9.cloned.1.call-done, bf16[3584,4096]{1,0:T(8,128)(2,1)} %constant_dynamic-update-slice_fusion, s32[]{:T(128)S(6)} %select_n.26, f32[256,3584]{1,0:T(8,128)} %get-tuple-element.13), kind=kOutput, calls=%fused_computation.28 | convolution fusion | flops 3767271424 | bytes 24903684 | tf_op jit(solution)/shard_map/dot_general | solution.py:20
  545.5 2.6 fusion.64
  548.1 2.1 convolution_multiply_fusion.14
  550.1 7.0 psum.80
  559.5 3.0 multiply_convert_fusion
  563.7 8.7 %fusion.2 = f32[256,2048]{1,0:T(8,128)} fusion(bf16[256,3584]{1,0:T(8,128)(2,1)S(1)} %get-tuple-element.16, bf16[3584,4096]{1,0:T(8,128)(2,1)} %constant_dynamic-update-slice_fusion, s32[]{:T(128)S(6)} %select_n.26), kind=kOutput, calls=%fused_computation.2 | convolution fusion | flops 3758096384 | bytes 18612228 | tf_op jit(solution)/shard_map/dot_general | solution.py:67
  574.5 2.1 fusion.109
  576.5 8.9 %psum.81 = bf16[256,16]{0,1:T(8,128)(2,1)S(1)} all-reduce(f32[256,16]{0,1:T(8,128)S(1)} %fusion.109), channel_id=1, replica_groups=mesh['client'=16,'tp'=2] {'tp'}, use_global_device_ids=true, to_apply=%region_8.9 | all-reduce | flops 4096 | bytes 24576 | tf_op jit(solution)/shard_map/psum | solution.py:72
  585.4 2.1 fusion.155
  587.9 17.9 %reduce-scatter.8.cloned.1.call-done = f32[256,1024]{1,0:T(8,128)} async-done(((f32[256,2048]{1,0:T(8,128)}), f32[256,1024]{1,0:T(8,128)}) %reduce-scatter.8.cloned.1.call-update) | async-done | bytes 1048592 | tf_op jit(solution)/shard_map/reduce_scatter | solution.py:71
  605.8 2.5 fusion.103
  609.3 20.5 %all-gather.11.cloned.1.call-done = bf16[256,2048]{1,0:T(8,128)(2,1)} async-done(((bf16[256,1024]{1,0:T(8,128)(2,1)}), bf16[256,2048]{1,0:T(8,128)(2,1)}) %all-gather.11.cloned.1.call-update) | async-done | bytes 1048592 | tf_op jit(solution)/shard_map/all_gather | solution.py:83
  629.8 1.6 fusion.94
  631.4 3.5 fusion.107
  636.0 12.3 %fusion.42 = bf16[256,3584]{1,0:T(8,128)(2,1)S(1)} fusion(f32[256,3584]{1,0:T(8,128)} %fusion.107, bf16[256,2048]{1,0:T(8,128)(2,1)} %all-gather.11.cloned.1.call-done, bf16[3584,4096]{1,0:T(8,128)(2,1)} %constant_dynamic-update-slice_fusion, s32[]{:T(128)S(6)} %select_n.26, f32[256,3584]{1,0:T(8,128)} %get-tuple-element.17), kind=kOutput, calls=%fused_computation.27 | convolution fusion | flops 3767271424 | bytes 24903684 | tf_op jit(solution)/shard_map/dot_general | solution.py:20
  650.0 7.0 psum.82
  657.0 2.1 fusion.78
  659.1 2.1 fusion.74
  661.2 32.9 %psum.84 = f32[1]{0:T(128)} all-reduce(f32[1]{0:T(128)} %convert_element_type.118), channel_id=1, replica_groups=mesh['client'=16,'tp'=2] {'client'}, use_global_device_ids=true, to_apply=%region_11.12 | all-reduce | flops 1 | bytes 8 | tf_op jit(solution)/shard_map/psum | solution.py:111
  694.8 60.0 %all-reduce.3.cloned.1.call-done = (f32[16,2048]{1,0:T(8,128)}, f32[16,3584]{1,0:T(8,128)}, f32[16,3584]{1,0:T(8,128)}, f32[16,2048]{1,0:T(8,128)}) async-done(((f32[16,2048]{1,0:T(8,128)}, f32[16,3584]{1,0:T(8,128)}, f32[16,3584]{1,0:T(8,128)}, f32[16,2048]{1,0:T(8,128)}), (f32[16,2048]{1,0:T(8,128)}, f32[16,3584]{1,0:T(8,128)}, f32[16,3584]{1,0:T(8,128)}, ...) | async-done | bytes 720912 | tf_op jit(solution)/shard_map/psum | solution.py:111
  754.8 1.8 broadcast_divide_fusion
  756.7 1.7 broadcast_divide_fusion.2
  (191 shorter events, 57.0 us)
Async XLA Ops:
  7.2 346.4 %all-gather.5.cloned.1.call-start = ((), (), s32[]{:S(2)}) async-start(), calls=%async_computation.3 | async-start | bytes 15597568 | tf_op jit(solution)/shard_map/all_gather | solution.py:45
  7.2 16.8 %collective-permute-start = (bf16[3584,128]{1,0:T(8,128)(2,1)}, bf16[3584,128]{1,0:T(8,128)(2,1)S(1)}, u32[]{:S(2)}, u32[]{:S(2)}) collective-permute-start(bf16[3584,128]{1,0:T(8,128)(2,1)} %param.14), channel_id=1, source_target_pairs={{0,2},{2,4},{4,6},{6,8},{8,10},{10,12},{12,14},{14,16},{16,18},{18... | collective-permute-start | bytes 2752520 | tf_op jit(solution)/shard_map/ppermute | solution.py:49
  24.0 15.6 %collective-permute-start.1 = (bf16[3584,128]{1,0:T(8,128)(2,1)S(1)}, bf16[3584,128]{1,0:T(8,128)(2,1)S(1)}, u32[]{:S(2)}, u32[]{:S(2)}) collective-permute-start(bf16[3584,128]{1,0:T(8,128)(2,1)S(1)} %collective-permute-done), channel_id=1, source_target_pairs={{0,2},{2,4},{4,6},{6,8},{8,10},{10,12},{12,14},{14,16},{16,18},{18... | collective-permute-start | bytes 2752520 | tf_op jit(solution)/shard_map/ppermute | solution.py:49
  24.1 381.9 %reduce-scatter.4.cloned.1.call-start = ((), (), s32[]{:S(2)}) async-start(), calls=%async_computation.4 | async-start | bytes 3145728 | tf_op jit(solution)/shard_map/reduce_scatter | solution.py:71
  39.7 35.3 %collective-permute-start.2 = (bf16[3584,128]{1,0:T(8,128)(2,1)S(1)}, bf16[3584,128]{1,0:T(8,128)(2,1)S(1)}, u32[]{:S(2)}, u32[]{:S(2)}) collective-permute-start(bf16[3584,128]{1,0:T(8,128)(2,1)S(1)} %collective-permute-done.1), channel_id=1, source_target_pairs={{0,2},{2,4},{4,6},{6,8},{8,10},{10,12},{12,14},{14,16},{16,18},{18... | collective-permute-start | bytes 2752520 | tf_op jit(solution)/shard_map/ppermute | solution.py:49
  75.0 255.3 %copy-start.7 = (bf16[3584,128]{1,0:T(8,128)(2,1)}, bf16[3584,128]{1,0:T(8,128)(2,1)S(1)}, u32[]{:S(2)}) copy-start(bf16[3584,128]{1,0:T(8,128)(2,1)S(1)} %collective-permute-done.2) | copy-start | bytes 2752516
  75.0 22.2 %collective-permute-start.3 = (bf16[3584,128]{1,0:T(8,128)(2,1)S(1)}, bf16[3584,128]{1,0:T(8,128)(2,1)S(1)}, u32[]{:S(2)}, u32[]{:S(2)}) collective-permute-start(bf16[3584,128]{1,0:T(8,128)(2,1)S(1)} %collective-permute-done.2), channel_id=1, source_target_pairs={{0,2},{2,4},{4,6},{6,8},{8,10},{10,12},{12,14},{14,16},{16,18},{18... | collective-permute-start | bytes 2752520 | tf_op jit(solution)/shard_map/ppermute | solution.py:49
  98.1 35.3 %collective-permute-start.4 = (bf16[3584,128]{1,0:T(8,128)(2,1)S(1)}, bf16[3584,128]{1,0:T(8,128)(2,1)S(1)}, u32[]{:S(2)}, u32[]{:S(2)}) collective-permute-start(bf16[3584,128]{1,0:T(8,128)(2,1)S(1)} %collective-permute-done.3), channel_id=1, source_target_pairs={{0,2},{2,4},{4,6},{6,8},{8,10},{10,12},{12,14},{14,16},{16,18},{18... | collective-permute-start | bytes 2752520 | tf_op jit(solution)/shard_map/ppermute | solution.py:49
  134.4 33.1 %collective-permute-start.5 = (bf16[3584,128]{1,0:T(8,128)(2,1)S(1)}, bf16[3584,128]{1,0:T(8,128)(2,1)S(1)}, u32[]{:S(2)}, u32[]{:S(2)}) collective-permute-start(bf16[3584,128]{1,0:T(8,128)(2,1)S(1)} %collective-permute-done.4), channel_id=1, source_target_pairs={{0,2},{2,4},{4,6},{6,8},{8,10},{10,12},{12,14},{14,16},{16,18},{18... | collective-permute-start | bytes 2752520 | tf_op jit(solution)/shard_map/ppermute | solution.py:49
  168.4 15.5 %collective-permute-start.6 = (bf16[3584,128]{1,0:T(8,128)(2,1)S(1)}, bf16[3584,128]{1,0:T(8,128)(2,1)S(1)}, u32[]{:S(2)}, u32[]{:S(2)}) collective-permute-start(bf16[3584,128]{1,0:T(8,128)(2,1)S(1)} %collective-permute-done.5), channel_id=1, source_target_pairs={{0,2},{2,4},{4,6},{6,8},{8,10},{10,12},{12,14},{14,16},{16,18},{18... | collective-permute-start | bytes 2752520 | tf_op jit(solution)/shard_map/ppermute | solution.py:49
  184.8 15.5 %collective-permute-start.7 = (bf16[3584,128]{1,0:T(8,128)(2,1)S(1)}, bf16[3584,128]{1,0:T(8,128)(2,1)S(1)}, u32[]{:S(2)}, u32[]{:S(2)}) collective-permute-start(bf16[3584,128]{1,0:T(8,128)(2,1)S(1)} %collective-permute-done.6), channel_id=1, source_target_pairs={{0,2},{2,4},{4,6},{6,8},{8,10},{10,12},{12,14},{14,16},{16,18},{18... | collective-permute-start | bytes 2752520 | tf_op jit(solution)/shard_map/ppermute | solution.py:49
  201.3 15.5 %collective-permute-start.8 = (bf16[3584,128]{1,0:T(8,128)(2,1)S(1)}, bf16[3584,128]{1,0:T(8,128)(2,1)S(1)}, u32[]{:S(2)}, u32[]{:S(2)}) collective-permute-start(bf16[3584,128]{1,0:T(8,128)(2,1)S(1)} %collective-permute-done.7), channel_id=1, source_target_pairs={{0,2},{2,4},{4,6},{6,8},{8,10},{10,12},{12,14},{14,16},{16,18},{18... | collective-permute-start | bytes 2752520 | tf_op jit(solution)/shard_map/ppermute | solution.py:49
  217.7 15.5 %collective-permute-start.9 = (bf16[3584,128]{1,0:T(8,128)(2,1)S(1)}, bf16[3584,128]{1,0:T(8,128)(2,1)S(1)}, u32[]{:S(2)}, u32[]{:S(2)}) collective-permute-start(bf16[3584,128]{1,0:T(8,128)(2,1)S(1)} %collective-permute-done.8), channel_id=1, source_target_pairs={{0,2},{2,4},{4,6},{6,8},{8,10},{10,12},{12,14},{14,16},{16,18},{18... | collective-permute-start | bytes 2752520 | tf_op jit(solution)/shard_map/ppermute | solution.py:49
  234.2 15.5 %collective-permute-start.10 = (bf16[3584,128]{1,0:T(8,128)(2,1)S(1)}, bf16[3584,128]{1,0:T(8,128)(2,1)S(1)}, u32[]{:S(2)}, u32[]{:S(2)}) collective-permute-start(bf16[3584,128]{1,0:T(8,128)(2,1)S(1)} %collective-permute-done.9), channel_id=1, source_target_pairs={{0,2},{2,4},{4,6},{6,8},{8,10},{10,12},{12,14},{14,16},{16,18},{18... | collective-permute-start | bytes 2752520 | tf_op jit(solution)/shard_map/ppermute | solution.py:49
  250.7 15.5 %collective-permute-start.11 = (bf16[3584,128]{1,0:T(8,128)(2,1)S(1)}, bf16[3584,128]{1,0:T(8,128)(2,1)S(1)}, u32[]{:S(2)}, u32[]{:S(2)}) collective-permute-start(bf16[3584,128]{1,0:T(8,128)(2,1)S(1)} %collective-permute-done.10), channel_id=1, source_target_pairs={{0,2},{2,4},{4,6},{6,8},{8,10},{10,12},{12,14},{14,16},{16,18},{18... | collective-permute-start | bytes 2752520 | tf_op jit(solution)/shard_map/ppermute | solution.py:49
  267.1 15.5 %collective-permute-start.12 = (bf16[3584,128]{1,0:T(8,128)(2,1)S(1)}, bf16[3584,128]{1,0:T(8,128)(2,1)S(1)}, u32[]{:S(2)}, u32[]{:S(2)}) collective-permute-start(bf16[3584,128]{1,0:T(8,128)(2,1)S(1)} %collective-permute-done.11), channel_id=1, source_target_pairs={{0,2},{2,4},{4,6},{6,8},{8,10},{10,12},{12,14},{14,16},{16,18},{18... | collective-permute-start | bytes 2752520 | tf_op jit(solution)/shard_map/ppermute | solution.py:49
  283.6 15.6 %collective-permute-start.13 = (bf16[3584,128]{1,0:T(8,128)(2,1)S(1)}, bf16[3584,128]{1,0:T(8,128)(2,1)}, u32[]{:S(2)}, u32[]{:S(2)}) collective-permute-start(bf16[3584,128]{1,0:T(8,128)(2,1)S(1)} %collective-permute-done.12), channel_id=1, source_target_pairs={{0,2},{2,4},{4,6},{6,8},{8,10},{10,12},{12,14},{14,16},{16,18},{18... | collective-permute-start | bytes 2752520 | tf_op jit(solution)/shard_map/ppermute | solution.py:49
  299.2 15.8 %collective-permute-start.14 = (bf16[3584,128]{1,0:T(8,128)(2,1)}, bf16[3584,128]{1,0:T(8,128)(2,1)}, u32[]{:S(2)}, u32[]{:S(2)}) collective-permute-start(bf16[3584,128]{1,0:T(8,128)(2,1)} %collective-permute-done.13), channel_id=1, source_target_pairs={{0,2},{2,4},{4,6},{6,8},{8,10},{10,12},{12,14},{14,16},{16,18},{18... | collective-permute-start | bytes 2752520 | tf_op jit(solution)/shard_map/ppermute | solution.py:49
  299.2 20.4 %copy-start.28 = (bf16[3584,128]{1,0:T(8,128)(2,1)S(1)}, bf16[3584,128]{1,0:T(8,128)(2,1)}, u32[]{:S(2)}) copy-start(bf16[3584,128]{1,0:T(8,128)(2,1)} %copy-done.27) | copy-start | bytes 2752516
  300.8 52.8 %copy-start.44 = (f32[256]{0:T(256)}, f32[256]{0:T(256)S(1)}, u32[]{:S(2)}) copy-start(f32[256]{0:T(256)S(1)} %add_rsqrt_fusion) | copy-start | bytes 3076
  300.8 19.9 %copy-start.26 = (bf16[3584,128]{1,0:T(8,128)(2,1)S(1)}, bf16[3584,128]{1,0:T(8,128)(2,1)}, u32[]{:S(2)}) copy-start(bf16[3584,128]{1,0:T(8,128)(2,1)} %copy-done.25) | copy-start | bytes 2752516
  302.6 58.4 %copy-start.38 = (bf16[256,16]{0,1:T(8,128)(2,1)}, bf16[256,16]{0,1:T(8,128)(2,1)S(1)}, u32[]{:S(2)}) copy-start(bf16[256,16]{0,1:T(8,128)(2,1)S(1)} %convolution_convert_fusion.2) | copy-start | bytes 24580
  302.6 19.1 %copy-start.24 = (bf16[3584,128]{1,0:T(8,128)(2,1)S(1)}, bf16[3584,128]{1,0:T(8,128)(2,1)}, u32[]{:S(2)}) copy-start(bf16[3584,128]{1,0:T(8,128)(2,1)} %copy-done.23) | copy-start | bytes 2752516
  317.3 5.5 copy-start.22
  319.6 4.3 copy-start.20
  320.7 4.2 copy-start.18
  321.7 4.2 copy-start.16
  322.8 4.3 copy-start.14
  323.9 4.2 copy-start.12
  324.9 4.3 copy-start.10
  329.2 4.3 copy-start.6
  345.3 4.1 copy-start.8
  349.4 4.2 copy-start.3
  349.4 4.2 copy-start.48
  353.6 7.4 copy-start.5
  361.0 3.1 copy-start.54
  364.2 9.5 %copy-start = (bf16[256,3584]{1,0:T(8,128)(2,1)}, bf16[256,3584]{1,0:T(8,128)(2,1)S(1)}, u32[]{:S(2)}) copy-start(bf16[256,3584]{1,0:T(8,128)(2,1)S(1)} %get-tuple-element.8) | copy-start | bytes 5505028
  364.2 9.5 %copy-start.32 = (f32[16,2048]{1,0:T(8,128)S(1)}, f32[16,2048]{1,0:T(8,128)}, u32[]{:S(2)}) copy-start(f32[16,2048]{1,0:T(8,128)} %param.18) | copy-start | bytes 393220
  364.2 9.5 %copy-start.4 = (f32[16,3584]{1,0:T(8,128)S(1)}, f32[16,3584]{1,0:T(8,128)}, u32[]{:S(2)}) copy-start(f32[16,3584]{1,0:T(8,128)} %param.17) | copy-start | bytes 688132
  373.6 56.2 %all-gather.7.cloned.1.call-start = ((), (), s32[]{:S(2)}) async-start(), calls=%async_computation.5 | async-start | bytes 1572864 | tf_op jit(solution)/shard_map/all_gather | solution.py:83
  385.9 48.0 %copy-start.37 = (bf16[256,16]{0,1:T(8,128)(2,1)}, bf16[256,16]{0,1:T(8,128)(2,1)S(1)}, u32[]{:S(2)}) copy-start(bf16[256,16]{0,1:T(8,128)(2,1)S(1)} %psum.77) | copy-start | bytes 24580
  408.4 94.2 %reduce-scatter.6.cloned.1.call-start = ((), (), s32[]{:S(2)}) async-start(), calls=%async_computation.6 | async-start | bytes 3145728 | tf_op jit(solution)/shard_map/reduce_scatter | solution.py:71
  433.8 12.3 %copy-start.39 = (bf16[256,16]{0,1:T(8,128)(2,1)S(1)}, bf16[256,16]{0,1:T(8,128)(2,1)}, u32[]{:S(2)}) copy-start(bf16[256,16]{0,1:T(8,128)(2,1)} %copy-done.38) | copy-start | bytes 24580
  446.2 8.7 %copy-start.45 = (f32[256]{0:T(256)S(1)}, f32[256]{0:T(256)}, u32[]{:S(2)}) copy-start(f32[256]{0:T(256)} %copy-done.44) | copy-start | bytes 3076
  446.2 8.6 %copy-start.49 = (f32[2048]{0:T(1024)S(1)}, f32[2048]{0:T(1024)}, u32[]{:S(2)}) copy-start(f32[2048]{0:T(1024)} %param.12) | copy-start | bytes 24580
  454.8 2.6 copy-start.33
  454.8 2.6 copy-start.55
  457.4 3.1 copy-start.42
  469.3 57.7 %all-gather.9.cloned.1.call-start = ((), (), s32[]{:S(2)}) async-start(), calls=%async_computation.7 | async-start | bytes 1572864 | tf_op jit(solution)/shard_map/all_gather | solution.py:83
  505.5 100.3 %reduce-scatter.8.cloned.1.call-start = ((), (), s32[]{:S(2)}) async-start(), calls=%async_computation.8 | async-start | bytes 3145728 | tf_op jit(solution)/shard_map/reduce_scatter | solution.py:71
  532.0 13.5 %copy-start.43 = (bf16[256,16]{0,1:T(8,128)(2,1)S(1)}, bf16[256,16]{0,1:T(8,128)(2,1)}, u32[]{:S(2)}) copy-start(bf16[256,16]{0,1:T(8,128)(2,1)} %copy-done.42) | copy-start | bytes 24580
  545.5 11.7 %copy-start.46 = (f32[256]{0:T(256)S(1)}, f32[256]{0:T(256)}, u32[]{:S(2)}) copy-start(f32[256]{0:T(256)} %copy-done.44) | copy-start | bytes 3076
  545.5 11.7 %copy-start.50 = (f32[2048]{0:T(1024)S(1)}, f32[2048]{0:T(1024)}, u32[]{:S(2)}) copy-start(f32[2048]{0:T(1024)} %param.12) | copy-start | bytes 24580
  558.7 3.8 copy-start.52
  559.5 3.0 copy-start.40
  572.4 57.4 %all-gather.11.cloned.1.call-start = ((), (), s32[]{:S(2)}) async-start(), calls=%async_computation.9 | async-start | bytes 1572864 | tf_op jit(solution)/shard_map/all_gather | solution.py:83
  608.2 26.7 %copy-start.2 = (bf16[256,3584]{1,0:T(8,128)(2,1)S(1)}, bf16[256,3584]{1,0:T(8,128)(2,1)}, u32[]{:S(2)}) copy-start(bf16[256,3584]{1,0:T(8,128)(2,1)} %copy-done.1) | copy-start | bytes 5505028
  608.3 146.5 %all-reduce.3.cloned.1.call-start = ((), (), s32[]{:S(2)}) async-start(), calls=%async_computation.10 | async-start | bytes 1441792 | tf_op jit(solution)/shard_map/psum | solution.py:111
  629.8 5.2 copy-start.31
  636.0 12.3 %copy-start.35 = (f32[16,3584]{1,0:T(8,128)S(1)}, f32[16,3584]{1,0:T(8,128)}, u32[]{:S(2)}) copy-start(f32[16,3584]{1,0:T(8,128)} %fusion.64) | copy-start | bytes 688132
  636.0 12.3 %copy-start.41 = (bf16[256,16]{0,1:T(8,128)(2,1)S(1)}, bf16[256,16]{0,1:T(8,128)(2,1)}, u32[]{:S(2)}) copy-start(bf16[256,16]{0,1:T(8,128)(2,1)} %copy-done.40) | copy-start | bytes 24580
  648.3 8.7 %copy-start.47 = (f32[256]{0:T(256)S(1)}, f32[256]{0:T(256)}, u32[]{:S(2)}) copy-start(f32[256]{0:T(256)} %copy-done.44) | copy-start | bytes 3076
  648.4 8.7 %copy-start.51 = (f32[2048]{0:T(1024)S(1)}, f32[2048]{0:T(1024)}, u32[]{:S(2)}) copy-start(f32[2048]{0:T(1024)} %param.12) | copy-start | bytes 24580
  649.4 9.7 %copy-start.36 = (f32[16,2048]{1,0:T(8,128)S(1)}, f32[16,2048]{1,0:T(8,128)}, u32[]{:S(2)}) copy-start(f32[16,2048]{1,0:T(8,128)} %get-tuple-element.15) | copy-start | bytes 393220
  (16 other events, 17.0 us)
Sparse Core Ops, SparseCore 0:
  24.2 137.5 all-gather.4
  373.7 32.1 reduce-scatter.3
  408.5 21.1 all-gather.6
  469.4 33.1 reduce-scatter.5
  505.6 21.3 all-gather.8
  572.5 33.1 reduce-scatter.7
  608.4 21.3 all-gather.10
  661.4 93.4 all-reduce.2
